TPU v7x, 32 devices: a whole 2x2x4 slice. The times are simulated.
32 devices in a mesh: zero: 16 (over z, x, core), tensor: 2 (over y).
Axes of the slice: x: 2, y: 2, z: 4, core: 2. Of those that a mesh axis runs over, the one named last changes fastest.
Arguments:
- grads: bfloat16 [16, 2, 16, 49152], P('zero', None, None, 'tensor'), may hold values from -1200 to 1200
- moment1: bfloat16 [2, 16, 49152], P(None, 'zero', 'tensor'), may hold values from -1 to 1
- moment2: float32 [2, 16, 49152], P(None, 'zero', 'tensor'), may hold values from 0.01 to 0.2
- master: float32 [2, 16, 49152], P(None, 'zero', 'tensor'), may hold values from -0.008 to 0.008
Outputs:
- new_moment1: bfloat16 [2, 16, 49152], P(None, 'zero', 'tensor')
- new_moment2: float32 [2, 16, 49152], P(None, 'zero', 'tensor')
- new_master: float32 [2, 16, 49152], P(None, 'zero', 'tensor')
- weights: bfloat16 [2, 16, 49152], P(None, None, 'tensor')
All inputs are finite; a program needn't handle non-finite values. Where the computation divides by a largest or mean magnitude, that divisor is 1e-20 or more.
Results may differ from a plain program's by a relative error of at most 0.0053.
Values may be sent and summed in bfloat16 or wider, within the bound.
A program may use at most 64 MiB of HBM per device.

v0:
```python
import jax
import jax.numpy as jnp
from jax import lax
from jax.sharding import PartitionSpec as P

decay_first = 0.9
decay_second = 0.95
learn_rate = 0.001
weight_decay = 0.1
adam_epsilon = 1e-08
peak_epsilon = 1e-06
bias_first = 1.0 - 0.9**10
bias_second = 1.0 - 0.95**10


def update_rows(gsum, moment1, moment2, master):
    new_moment1 = (decay_first * moment1.astype(jnp.float32) + (1.0 - decay_first) * gsum).astype(
        jnp.bfloat16
    )
    new_moment2 = decay_second * moment2 + (1.0 - decay_second) * gsum * gsum
    stored = lax.optimization_barrier(new_moment1).astype(jnp.float32)
    step_dir = stored / bias_first / (jnp.sqrt(new_moment2 / bias_second) + adam_epsilon)
    new_master = master - learn_rate * (step_dir + weight_decay * master)
    local_peak = jnp.max(jnp.abs(new_master), axis=(1, 2))
    wpeak = lax.pmax(local_peak, ("zero", "tensor")) + peak_epsilon
    normed = (new_master / wpeak[:, None, None]).astype(jnp.bfloat16)
    weights = lax.all_gather(normed, "zero", axis=1, tiled=True)
    return (new_moment1, new_moment2, new_master, weights)


def local(grads, moment1, moment2, master):
    local_peak = jnp.max(jnp.abs(grads), axis=(0, 2, 3)).astype(jnp.float32)
    peak = lax.pmax(local_peak, ("zero", "tensor")) + peak_epsilon
    scaled_half = (grads.astype(jnp.float32) / peak[None, :, None, None]).astype(jnp.bfloat16)
    received = lax.all_to_all(scaled_half, "zero", split_axis=2, concat_axis=0, tiled=True)
    gsum = jnp.sum(received.astype(jnp.float32), axis=0)
    return update_rows(gsum, moment1, moment2, master)


def solution(mesh):
    placed = (
        P("zero", None, None, "tensor"),
        P(None, "zero", "tensor"),
        P(None, "zero", "tensor"),
        P(None, "zero", "tensor"),
    )
    return jax.shard_map(
        local,
        mesh=mesh,
        in_specs=placed,
        out_specs=(
            P(None, "zero", "tensor"),
            P(None, "zero", "tensor"),
            P(None, "zero", "tensor"),
            P(None, None, "tensor"),
        ),
        check_vma=False,
    )
```

profile of v0, /device:TPU:0, one launch (start us, length us, event | category | flops | bytes accessed | tf_op | source)
XLA Modules:
  0.0 187.2 jit_solution(13088254821506365265)
XLA Ops:
  7.2 0.0 copy-start
  7.2 0.0 all-gather.2.cloned.1.call-start
  7.2 1.8 abs_reduce_fusion
  9.0 42.0 %pmax.14 = f32[2]{0:T(128)S(1)} all-reduce(bf16[2]{0:T(256)(128)(2,1)S(1)} %abs_reduce_fusion), channel_id=1, replica_groups=mesh['zero'=16,'tensor'=2] {'zero','tensor'}, use_global_device_ids=true, to_apply=%region_1.0 | all-reduce | flops 2 | bytes 12 | tf_op jit(solution)/shard_map/pmax | solution.py:33
  51.0 0.0 copy-done
  51.0 0.3 divide_convert_fusion
  51.3 1.6 copy.17
  52.9 41.1 %all_to_all.4 = bf16[1,2,16,24576]{3,1,0,2:T(2,128)(2,1)S(1)} all-to-all(bf16[1,2,16,24576]{3,1,0,2:T(2,128)(2,1)S(1)} %copy.17), channel_id=1, replica_groups=mesh['zero'=16,'tensor'=2] {'zero'}, dimensions={2} | all-to-all | bytes 3145728 | tf_op jit(solution)/shard_map/all_to_all | solution.py:35
  94.1 0.0 copy-start.4
  94.1 0.0 copy-start.2
  94.1 0.0 copy-start.3
  94.1 1.4 convert_reduce_fusion
  95.4 0.0 copy-done.4
  95.4 0.2 fusion.2
  95.6 0.0 copy-done.2
  95.6 0.0 copy-done.3
  95.6 0.0 copy-start.1
  95.6 0.8 abs_reduce_fusion.1
  96.5 40.1 %pmax.15 = f32[2]{0:T(128)S(1)} all-reduce(f32[2]{0:T(128)S(1)} %get-tuple-element.16), channel_id=1, replica_groups=mesh['zero'=16,'tensor'=2] {'zero','tensor'}, use_global_device_ids=true, to_apply=%region_4.0 | all-reduce | flops 2 | bytes 16 | tf_op jit(solution)/shard_map/pmax | solution.py:25
  136.6 0.8 divide_convert_fusion.1
  137.4 0.0 all-gather.2.cloned.1.call-update
  137.4 0.9 copy.22
  138.3 0.9 copy.21
  139.2 37.7 %all-gather.2.cloned.1.call-done = bf16[2,16,24576]{2,0,1:T(2,128)(2,1)} async-done(((bf16[2,1,24576]{2,0,1:T(2,128)(2,1)}), bf16[2,16,24576]{2,0,1:T(2,128)(2,1)}) %all-gather.2.cloned.1.call-update) | async-done | bytes 1572880 | tf_op jit(solution)/shard_map/all_gather | solution.py:27
  176.9 3.4 %copy.23 = bf16[2,16,24576]{2,1,0:T(8,128)(2,1)} copy(bf16[2,16,24576]{2,0,1:T(2,128)(2,1)} %all-gather.2.cloned.1.call-done) | data formatting | bytes 3145728
  180.3 0.0 copy-done.1
  (2 shorter events, 0.0 us)
Async XLA Ops:
  7.2 43.8 %copy-start = (bf16[1,2,16,24576]{3,2,1,0:T(8,128)(2,1)S(1)}, bf16[1,2,16,24576]{3,2,1,0:T(8,128)(2,1)}, u32[]{:S(2)}) copy-start(bf16[1,2,16,24576]{3,2,1,0:T(8,128)(2,1)} %param.4) | copy-start | bytes 4718596
  7.2 169.7 %all-gather.2.cloned.1.call-start = ((), (), s32[]{:S(2)}) async-start(), calls=%async_computation.1 | async-start | bytes 1671168 | tf_op jit(solution)/shard_map/all_gather | solution.py:27
  94.1 1.4 copy-start.4
  94.1 1.6 copy-start.2
  94.1 1.6 copy-start.3
  95.6 84.7 %copy-start.1 = (bf16[2,1,24576]{2,0,1:T(2,128)(2,1)}, bf16[2,1,24576]{2,0,1:T(2,128)(2,1)S(1)}, u32[]{:S(2)}) copy-start(bf16[2,1,24576]{2,0,1:T(2,128)(2,1)S(1)} %fusion.2) | copy-start | bytes 294916
Sparse Core Ops, SparseCore 0:
  137.5 39.3 all-gather.1
where the time goes:
time: 188 us; the launch traced here: 187 us
  blocking collectives  123 us (65%)
  waiting for transfers between devices  37.8 us (20%)
  between operations  14.1 us (8%)
  local copies, waits for them, and re-layouts  6.81 us (4%)
  other arithmetic  5.24 us (3%)
    pmax x1, blocking collectives, local(): peak = lax.pmax(local_peak, ('zero', 'tensor')) + peak_epsilon  42 us
    all_to_all x1, blocking collectives, local(): lax.all_to_all(scaled_half, 'zero', split_axis=2, concat_axis=0, tiled=True)  41.1 us
    pmax x1, blocking collectives, update_rows(): wpeak = lax.pmax(local_peak, ('zero', 'tensor')) + peak_epsilon  40.1 us
    all_gather x1, waiting for transfers between devices, update_rows(): weights = lax.all_gather(normed, 'zero', axis=1, tiled=True)  37.7 us
    unnamed x13, local copies, waits for them, and re-layouts  5.2 us
  transfers between devices with their start and end apart: 1, of which 1 were waited for; matrix products, arithmetic and copies ran while one was open for 1% of the time, Pallas kernels for 0%

commit v1 on v0

v1 whole, which is shorter than its diff:
```python
import functools

import jax
import jax.numpy as jnp
from jax import lax
from jax.experimental import pallas as pl
from jax.experimental.pallas import tpu as pltpu
from jax.sharding import PartitionSpec as P

decay_first = 0.9
decay_second = 0.95
learn_rate = 0.001
weight_decay = 0.1
adam_epsilon = 1e-08
peak_epsilon = 1e-06
bias_first = 1.0 - 0.9**10
bias_second = 1.0 - 0.95**10

LANES = 128
MESH = pl.DeviceIdType.MESH
f32 = jnp.float32
bf16 = jnp.bfloat16


def split_zero(n):
    nc = 2 if n % 2 == 0 else 1
    m = n // nc
    nx = 1
    while (nx * 2) * (nx * 2) <= m and m % (nx * 2) == 0:
        nx *= 2
    return m // nx, nx, nc


def fold(block):
    return jnp.max(jnp.abs(block.astype(f32)).reshape(-1, 8, LANES), axis=0)


def kernel(dims, g_ref, m1_ref, m2_ref, ms_ref,
           o1_ref, o2_ref, om_ref, wg_ref, wp_ref,
           buf_c, send_x, buf_x, send_z, buf_z, own,
           pk, pk_in, wk, wk_in,
           cs, cr, xs, xr, zs, zr, gzs, gzr, gxs, gxr, gcs, gcr, ps, pr, ws, wr):
    nz, nx, nc, nt, nl = dims
    me = lax.axis_index("zero")
    te = lax.axis_index("tensor")
    c = lax.rem(me, nc)
    x = lax.rem(lax.div(me, nc), nx)
    z = lax.div(me, nc * nx)

    def at(zz, xx, cc):
        return {"zero": (zz * nx + xx) * nc + cc}

    def turn(v, d, n):
        return lax.rem(v + d, n)

    core_peers = [at(z, x, turn(c, d, nc)) for d in range(1, nc)]
    x_peers = [at(z, turn(x, d, nx), c) for d in range(1, nx)]
    z_peers = [at(turn(z, d, nz), x, c) for d in range(1, nz)]
    t_peers = [{"tensor": turn(te, d, nt)} for d in range(1, nt)]
    groups = [p for p in (core_peers, x_peers, z_peers, t_peers) if p]
    pending = []

    def send(src, dst, s, r, to):
        copy = pltpu.make_async_remote_copy(
            src_ref=src, dst_ref=dst, send_sem=s, recv_sem=r,
            device_id=to, device_id_type=MESH)
        copy.start()
        pending.append(copy)

    def arrived(dst, r):
        pltpu.make_async_copy(dst, dst, r).wait()

    barrier = pltpu.get_barrier_semaphore()
    everyone = [p for g in groups for p in g]
    for p in everyone:
        pl.semaphore_signal(barrier, inc=1, device_id=p, device_id_type=MESH)

    class Peak:
        def __init__(self, held, inbox, s, r):
            self.held, self.inbox, self.s, self.r = held, inbox, s, r
            self.stage = 0
            self.slot = 0

        def push(self):
            for i, p in enumerate(groups[self.stage]):
                k = self.slot + i
                send(self.held.at[self.stage], self.inbox.at[k], self.s.at[k], self.r.at[k], p)

        def pull(self):
            best = self.held[self.stage]
            for i in range(len(groups[self.stage])):
                k = self.slot + i
                arrived(self.inbox.at[k], self.r.at[k])
                best = jnp.maximum(best, self.inbox[k])
            self.slot += len(groups[self.stage])
            self.stage += 1
            self.held[self.stage] = best
            if self.stage < len(groups):
                self.push()

        def step(self):
            if self.stage < len(groups):
                self.pull()

        def finish(self):
            while self.stage < len(groups):
                self.pull()
            return [jnp.max(self.held[self.stage, l]) + peak_epsilon for l in range(nl)]

    for l in range(nl):
        def part(i, best, l=l):
            zz, rest = lax.div(i, nx * nc), lax.rem(i, nx * nc)
            return jnp.maximum(best, fold(g_ref[zz, lax.div(rest, nc), lax.rem(rest, nc), l]))
        pk[0, l] = lax.fori_loop(0, nz * nx * nc, part, jnp.zeros((8, LANES), f32))

    pl.semaphore_wait(barrier, len(everyone))

    order = [(d, l) for d in list(range(1, nz)) + [0] for l in range(nl)]
    other = [turn(c, d, nc) for d in range(1, nc)]
    for d, l in order:
        zz = turn(z, d, nz)
        for i, cc in enumerate(other):
            send(g_ref.at[zz, :, cc, l], buf_c.at[i, d, l], cs.at[i, d, l], cr.at[i, d, l], core_peers[i])
    peak = Peak(pk, pk_in, ps, pr)
    peak.push()

    def pair(d, l, xx):
        total = g_ref[turn(z, d, nz), xx, c, l].astype(f32)
        for i in range(nc - 1):
            total = total + buf_c[i, d, l, xx].astype(f32)
        return total

    for k, (d, l) in enumerate(order):
        for i in range(nc - 1):
            arrived(buf_c.at[i, d, l], cr.at[i, d, l])
        for e in range(1, nx):
            send_x[e - 1, d, l] = pair(d, l, turn(x, e, nx)).astype(bf16)
            send(send_x.at[e - 1, d, l], buf_x.at[e - 1, d, l],
                 xs.at[e - 1, d, l], xr.at[e - 1, d, l], x_peers[e - 1])
    peak.step()
    for k, (d, l) in enumerate(order):
        for e in range(1, nx):
            arrived(buf_x.at[e - 1, d, l], xr.at[e - 1, d, l])
        total = pair(d, l, x)
        for e in range(1, nx):
            total = total + buf_x[e - 1, d, l].astype(f32)
        if d:
            send_z[d - 1, l] = total.astype(bf16)
            send(send_z.at[d - 1, l], buf_z.at[d - 1, l], zs.at[d - 1, l], zr.at[d - 1, l], z_peers[d - 1])
        else:
            own[l] = total
        if l == nl - 1:
            peak.step()
    peaks = peak.finish()

    for l in range(nl):
        total = own[l]
        for d in range(1, nz):
            arrived(buf_z.at[d - 1, l], zr.at[d - 1, l])
            total = total + buf_z[d - 1, l].astype(f32)
        gsum = total / peaks[l]
        first = (decay_first * m1_ref[l].astype(f32) + (1.0 - decay_first) * gsum).astype(bf16)
        second = decay_second * m2_ref[l] + (1.0 - decay_second) * gsum * gsum
        o1_ref[l] = first
        o2_ref[l] = second
        step_dir = first.astype(f32) / bias_first / (jnp.sqrt(second / bias_second) + adam_epsilon)
        master = ms_ref[l]
        fresh = master - learn_rate * (step_dir + weight_decay * master)
        om_ref[l] = fresh
        wg_ref[z, x, c, l] = fresh.astype(bf16)
        wk[0, l] = fold(fresh)
        mine = wg_ref.at[z, x, c, l]
        for d in range(1, nz):
            send(mine, mine, gzs.at[d - 1, l], gzr.at[d - 1, l], z_peers[d - 1])
        for e in range(1, nx):
            send(mine, mine, gxs.at[e - 1, 0, l], gxr.at[e - 1, 0, l], x_peers[e - 1])
        for i in range(1, nc):
            send(mine, mine, gcs.at[i - 1, 0, 0, l], gcr.at[i - 1, 0, 0, l], core_peers[i - 1])
    wpeak = Peak(wk, wk_in, ws, wr)
    wpeak.push()

    def back(v, d, n):
        return lax.rem(v + n - d, n)

    def from_z(d, l):
        block = wg_ref.at[back(z, d, nz), x, c, l]
        arrived(block, gzr.at[d - 1, l])
        for e in range(1, nx):
            send(block, block, gxs.at[e - 1, d, l], gxr.at[e - 1, d, l], x_peers[e - 1])
        for i in range(1, nc):
            send(block, block, gcs.at[i - 1, 0, d, l], gcr.at[i - 1, 0, d, l], core_peers[i - 1])

    def from_x(d, l):
        for e in range(1, nx):
            block = wg_ref.at[back(z, d, nz), back(x, e, nx), c, l]
            arrived(block, gxr.at[e - 1, d, l])
            for i in range(1, nc):
                send(block, block, gcs.at[i - 1, e, d, l], gcr.at[i - 1, e, d, l], core_peers[i - 1])

    wpeak.step()
    for d in range(1, nz):
        for l in range(nl):
            from_z(d, l)
        if d == 1:
            wpeak.step()
        for l in range(nl):
            from_x(d - 1, l)
    wpeak.step()
    for l in range(nl):
        from_x(nz - 1, l)
    peaks = wpeak.finish()
    for l in range(nl):
        wp_ref[l] = jnp.full((8, LANES), peaks[l], f32)
    for d in range(nz):
        for e in range(nx):
            for l in range(nl):
                for i in range(1, nc):
                    block = wg_ref.at[back(z, d, nz), back(x, e, nx), back(c, i, nc), l]
                    arrived(block, gcr.at[i - 1, e, d, l])
    for copy in pending:
        copy.wait_send()


def local(n, nt, grads, moment1, moment2, master):
    nz, nx, nc = split_zero(n)
    nl, rows, width = grads.shape[1:]
    deep = (rows // n) * width // LANES
    dims = (nz, nx, nc, nt, nl)
    g = grads.reshape(nl, n, deep, LANES).transpose(1, 0, 2, 3).reshape(nz, nx, nc, nl, deep, LANES)
    flat = (nl, deep, LANES)
    peers = (nc - 1) + (nx - 1) + (nz - 1) + (nt - 1)
    stages = sum(k > 1 for k in (nc, nx, nz, nt))
    c1, x1, z1 = max(nc - 1, 1), max(nx - 1, 1), max(nz - 1, 1)
    dma = pltpu.SemaphoreType.DMA
    tile = (nl, 8, LANES)
    vm = pl.BlockSpec(memory_space=pltpu.VMEM)
    sems = [dma((c1, nz, nl))] * 2 + [dma((x1, nz, nl))] * 2 + [dma((z1, nl))] * 2
    sems += [dma((z1, nl))] * 2 + [dma((x1, nz, nl))] * 2 + [dma((c1, nx, nz, nl))] * 2
    sems += [dma((peers,))] * 4
    o1, o2, om, wg, wp = pl.pallas_call(
        functools.partial(kernel, dims),
        out_shape=(
            jax.ShapeDtypeStruct(flat, bf16),
            jax.ShapeDtypeStruct(flat, f32),
            jax.ShapeDtypeStruct(flat, f32),
            jax.ShapeDtypeStruct((nz, nx, nc) + flat, bf16),
            jax.ShapeDtypeStruct(tile, f32),
        ),
        in_specs=[vm] * 4,
        out_specs=(vm,) * 5,
        scratch_shapes=[
            pltpu.VMEM((c1, nz, nl, nx, deep, LANES), bf16),
            pltpu.VMEM((x1, nz) + flat, bf16),
            pltpu.VMEM((x1, nz) + flat, bf16),
            pltpu.VMEM((z1,) + flat, bf16),
            pltpu.VMEM((z1,) + flat, bf16),
            pltpu.VMEM(flat, f32),
            pltpu.VMEM((stages + 1,) + tile, f32),
            pltpu.VMEM((peers,) + tile, f32),
            pltpu.VMEM((stages + 1,) + tile, f32),
            pltpu.VMEM((peers,) + tile, f32),
        ] + sems,
        compiler_params=pltpu.CompilerParams(collective_id=0, has_side_effects=True),
    )(g, moment1.reshape(flat), moment2.reshape(flat), master.reshape(flat))
    wg = wg.reshape((n,) + flat).astype(f32) / wp[:, :1, :1][None]
    weights = wg.astype(bf16).transpose(1, 0, 2, 3).reshape(nl, rows, width)
    shape = moment1.shape
    return o1.reshape(shape), o2.reshape(shape), om.reshape(shape), weights


def solution(mesh):
    n, nt = mesh.shape["zero"], mesh.shape["tensor"]
    placed = (
        P("zero", None, None, "tensor"),
        P(None, "zero", "tensor"),
        P(None, "zero", "tensor"),
        P(None, "zero", "tensor"),
    )
    return jax.shard_map(
        functools.partial(local, n, nt),
        mesh=mesh,
        in_specs=placed,
        out_specs=(
            P(None, "zero", "tensor"),
            P(None, "zero", "tensor"),
            P(None, "zero", "tensor"),
            P(None, None, "tensor"),
        ),
        check_vma=False,
    )
```

time: 188 us -> 58.3 us (0.31)
  blocking collectives: 123 us -> 0 us
  Pallas kernels: 0 us -> 44.7 us
  waiting for transfers between devices: 37.8 us -> 0 us
  between operations: 14.1 us -> 0.68 us
  local copies, waits for them, and re-layouts: 6.81 us -> 10.7 us
  other arithmetic: 5.24 us -> 1.91 us
    pmax x2 -> x0, blocking collectives: 82.1 us -> none  [the longest x1 42 us: local(): peak = lax.pmax(local_peak, ('zero', 'tensor')) + peak_epsilon]
    pallas_call x0 -> x1, Pallas kernels: none -> 44.7 us  [local(): pl.pallas_call(functools.partial(kernel, dims), out_shape=(jax.ShapeDtype...]
    all_to_all x1 -> x0, blocking collectives: 41.1 us -> none  [local(): lax.all_to_all(scaled_half, 'zero', split_axis=2, concat_axis=0, tiled=True)]
    all_gather x1 -> x0, waiting for transfers between devices: 37.7 us -> none  [update_rows(): weights = lax.all_gather(normed, 'zero', axis=1, tiled=True)]
    reshape x0 -> x4, local copies, waits for them, and re-layouts: none -> 5.24 us  [the longest x2 2.4 us: local(): weights = wg.astype(bf16).transpose(1, 0, 2, 3).reshape(nl, rows, width)]
    reduce_max x2 -> x0, other arithmetic: 2.6 us -> none  [the longest x1 1.77 us: local(): local_peak = jnp.max(jnp.abs(grads), axis=(0, 2, 3)).astype(jnp.float32)]
    transpose x0 -> x1, other arithmetic: none -> 1.91 us  [local(): weights = wg.astype(bf16).transpose(1, 0, 2, 3).reshape(nl, rows, width)]
    unnamed x13 -> x8, local copies, waits for them, and re-layouts: 5.2 us -> 4.67 us
  transfers between devices with their start and end apart: 1 -> 0, of which waited for: 1 -> 0; matrix products, arithmetic and copies ran while one was open for 1% -> 0% of each run, Pallas kernels for 0% -> 0%
where the time goes in v1:
time: 58.3 us; the launch traced here: 58 us
  Pallas kernels  44.7 us (77%)
  local copies, waits for them, and re-layouts  10.7 us (18%)
  other arithmetic  1.91 us (3%)
  between operations  0.68 us (1%)
    pallas_call x1, Pallas kernels, local(): pl.pallas_call(functools.partial(kernel, dims), out_shape=(jax.ShapeDtype...  44.7 us
    unnamed x8, local copies, waits for them, and re-layouts  4.67 us
    reshape x2, local copies, waits for them, and re-layouts, local(): weights = wg.astype(bf16).transpose(1, 0, 2, 3).reshape(nl, rows, width)  2.4 us
    transpose x1, other arithmetic, local(): weights = wg.astype(bf16).transpose(1, 0, 2, 3).reshape(nl, rows, width)  1.91 us
    reshape x1, local copies, waits for them, and re-layouts, local(): return (o1.reshape(shape), o2.reshape(shape), om.reshape(shape), weights)  1.56 us
    reshape x1, local copies, waits for them, and re-layouts, local(): grads.reshape(nl, n, deep, LANES).transpose(1, 0, 2, 3)  1.27 us

profile of v1, /device:TPU:0, one launch (start us, length us, event | category | flops | bytes accessed | tf_op | source)
XLA Modules:
  0.0 58.0 jit_solution(7925199885728931337)
XLA Ops:
  0.6 1.5 %copy.20 = bf16[1,2,192,128]{3,2,1,0:T(8,128)(2,1)} copy(bf16[1,2,192,128]{3,1,2,0:T(2,128)(2,1)} %bitcast.35) | data formatting | bytes 196608
  2.2 1.8 %copy.17 = bf16[4,8,192,128]{3,2,1,0:T(8,128)(2,1)S(1)} copy(bf16[4,8,192,128]{3,1,2,0:T(8,128)(2,1)} %bitcast.29) | data formatting | bytes 3145728
  3.9 1.3 %copy.12 = bf16[2,16,192,128]{3,2,0,1:T(8,128)(2,1)} copy(bf16[2,16,192,128]{3,2,1,0:T(8,128)(2,1)S(1)} %bitcast.28) | data formatting | bytes 3145728 | tf_op jit(solution)/shard_map/reshape | solution.py:229
  5.2 44.7 %shard_map.75 = (bf16[2,192,128]{2,1,0:T(8,128)(2,1)}, f32[2,192,128]{2,1,0:T(8,128)}, f32[2,192,128]{2,1,0:T(8,128)}, bf16[4,2,2,2,192,128]{5,4,3,2,1,0:T(8,128)(2,1)}, f32[2,8,128]{2,1,0:T(8,128)}) custom-call(bf16[4,2,2,2,192,128]{5,4,3,2,1,0:T(8,128)(2,1)} %bitcast.27, bf16[2,192,128]{2,1,0:T(8,128)(2,1)} %bitcast.30, f32[2,192,128]{2,1,0:T(8,128)} %bitcast.33, ...), custom_call_target="tpu_custom_call" | custom-call | tf_op jit(solution)/shard_map/pallas_call | solution.py:240
  49.9 1.6 %reshape.44 = bf16[2,1,24576]{2,0,1:T(2,128)(2,1)} reshape(bf16[2,192,128]{2,1,0:T(8,128)(2,1)} %get-tuple-element.9) | data formatting | bytes 196608 | tf_op jit(solution)/shard_map/reshape | solution.py:268
  51.5 0.8 %slice_reduce_fusion = f32[2]{0:T(128)S(1)} fusion(f32[2,8,128]{2,1,0:T(8,128)} %get-tuple-element.13), kind=kLoop, calls=%fused_computation.4 | loop fusion | bytes 16 | tf_op jit(solution)/shard_map/slice | solution.py:265
  52.3 1.9 %fusion.1 = bf16[2,16,192,128]{3,2,0,1:T(8,128)(2,1)S(1)} fusion(bf16[4,2,2,2,192,128]{5,4,3,2,1,0:T(8,128)(2,1)} %get-tuple-element.12, f32[2]{0:T(128)S(1)} %slice_reduce_fusion), kind=kLoop, calls=%fused_computation.2 | loop fusion | flops 2359296 | bytes 3145736 | tf_op jit(solution)/shard_map/transpose | solution.py:266
  54.2 0.4 reshape.49
  54.6 0.0 copy-start.1
  54.6 0.0 copy-start
  54.6 2.0 %copy.16 = bf16[2,16,24576]{2,1,0:T(8,128)(2,1)} copy(bf16[2,16,24576]{2,0,1:T(2,128)(2,1)S(1)} %reshape.49) | data formatting | bytes 3145728 | tf_op jit(solution)/shard_map/reshape | solution.py:266
  56.6 0.0 copy-done.1
  56.6 0.7 %copy.23 = f32[2,1,24576]{2,1,0:T(1,128)} copy(f32[2,1,24576]{2,1,0:T(1,128)S(1)} %bitcast.32) | data formatting | bytes 393216
  57.3 0.0 copy-done
  57.3 0.7 %copy.24 = f32[2,1,24576]{2,1,0:T(1,128)} copy(f32[2,1,24576]{2,1,0:T(1,128)S(1)} %bitcast.31) | data formatting | bytes 393216
Async XLA Ops:
  54.6 2.0 %copy-start.1 = (f32[2,192,128]{2,1,0:T(8,128)S(1)}, f32[2,192,128]{2,1,0:T(8,128)}, u32[]{:S(2)}) copy-start(f32[2,192,128]{2,1,0:T(8,128)} %get-tuple-element.10) | copy-start | bytes 589828
  54.6 2.7 %copy-start = (f32[2,192,128]{2,1,0:T(8,128)S(1)}, f32[2,192,128]{2,1,0:T(8,128)}, u32[]{:S(2)}) copy-start(f32[2,192,128]{2,1,0:T(8,128)} %get-tuple-element.11) | copy-start | bytes 589828

commit v2 on v1

v2 whole, which is shorter than its diff:
```python
import functools

import jax
import jax.numpy as jnp
from jax import lax
from jax.experimental import pallas as pl
from jax.experimental.pallas import tpu as pltpu
from jax.sharding import PartitionSpec as P

decay_first = 0.9
decay_second = 0.95
learn_rate = 0.001
weight_decay = 0.1
adam_epsilon = 1e-08
peak_epsilon = 1e-06
bias_first = 1.0 - 0.9**10
bias_second = 1.0 - 0.95**10

LANES = 128
MESH = pl.DeviceIdType.MESH
f32 = jnp.float32
bf16 = jnp.bfloat16


def split_zero(n):
    nc = 2 if n % 2 == 0 else 1
    m = n // nc
    nx = 1
    while (nx * 2) * (nx * 2) <= m and m % (nx * 2) == 0:
        nx *= 2
    return m // nx, nx, nc


def fold(block):
    return jnp.max(jnp.abs(block.astype(f32)).reshape(-1, 8, LANES), axis=0)


def kernel(dims, g_ref, m1_ref, m2_ref, ms_ref,
           o1_ref, o2_ref, om_ref, ow_ref,
           wg, m1_wide, o1_wide, buf_c, send_x, buf_x, send_z, buf_z, own,
           pk, pk_in, wk, wk_in,
           cs, cr, xs, xr, zs, zr, gzs, gzr, gxs, gxr, gcs, gcr, ps, pr, ws, wr):
    nz, nx, nc, nt, nl = dims
    me = lax.axis_index("zero")
    te = lax.axis_index("tensor")
    c = lax.rem(me, nc)
    x = lax.rem(lax.div(me, nc), nx)
    z = lax.div(me, nc * nx)

    def at(zz, xx, cc):
        return {"zero": (zz * nx + xx) * nc + cc}

    def turn(v, d, n):
        return lax.rem(v + d, n)

    core_peers = [at(z, x, turn(c, d, nc)) for d in range(1, nc)]
    x_peers = [at(z, turn(x, d, nx), c) for d in range(1, nx)]
    z_peers = [at(turn(z, d, nz), x, c) for d in range(1, nz)]
    t_peers = [{"tensor": turn(te, d, nt)} for d in range(1, nt)]
    near = core_peers + t_peers + [
        {**at(z, x, turn(c, i, nc)), "tensor": turn(te, d, nt)} for i in range(1, nc) for d in range(1, nt)]
    far = [at(turn(z, d, nz), turn(x, e, nx), c) for d in range(nz) for e in range(nx) if d or e]
    pending = []

    def send(src, dst, s, r, to):
        copy = pltpu.make_async_remote_copy(
            src_ref=src, dst_ref=dst, send_sem=s, recv_sem=r,
            device_id=to, device_id_type=MESH)
        copy.start()
        pending.append(copy)

    def arrived(dst, r):
        pltpu.make_async_copy(dst, dst, r).wait()

    barrier = pltpu.get_barrier_semaphore()
    everyone = near + far
    for p in everyone:
        pl.semaphore_signal(barrier, inc=1, device_id=p, device_id_type=MESH)

    class Peak:
        def __init__(self, held, inbox, s, r):
            self.held, self.inbox, self.s, self.r = held, inbox, s, r

        def push(self, stage):
            first = 0 if stage == 0 else len(near)
            for i, p in enumerate(near if stage == 0 else far):
                k = first + i
                send(self.held.at[stage], self.inbox.at[k], self.s.at[k], self.r.at[k], p)

        def pull(self, stage):
            first = 0 if stage == 0 else len(near)
            best = self.held[stage]
            for k in range(first, first + len(near if stage == 0 else far)):
                arrived(self.inbox.at[k], self.r.at[k])
                best = jnp.maximum(best, self.inbox[k])
            return best

        def relay(self):
            self.held[1] = self.pull(0)
            self.push(1)

        def finish(self):
            best = self.pull(1)
            return [jnp.max(best[l]) + peak_epsilon for l in range(nl)]

    for l in range(nl):
        def part(i, best, l=l):
            zz, rest = lax.div(i, nx * nc), lax.rem(i, nx * nc)
            return jnp.maximum(best, fold(g_ref[l, zz, lax.div(rest, nc), lax.rem(rest, nc)]))
        pk[0, l] = lax.fori_loop(0, nz * nx * nc, part, jnp.zeros((8, LANES), f32))

    pl.semaphore_wait(barrier, len(everyone))

    peak = Peak(pk, pk_in, ps, pr)
    peak.push(0)
    order = [(d, l) for d in list(range(1, nz)) + [0] for l in range(nl)]
    other = [turn(c, d, nc) for d in range(1, nc)]
    for d, l in order:
        zz = turn(z, d, nz)
        for i, cc in enumerate(other):
            send(g_ref.at[l, zz, :, cc], buf_c.at[i, d, l], cs.at[i, d, l], cr.at[i, d, l], core_peers[i])
    m1_wide[...] = m1_ref[...].astype(f32)

    def pair(d, l, xx):
        total = g_ref[l, turn(z, d, nz), xx, c].astype(f32)
        for i in range(nc - 1):
            total = total + buf_c[i, d, l, xx].astype(f32)
        return total

    for k, (d, l) in enumerate(order):
        for i in range(nc - 1):
            arrived(buf_c.at[i, d, l], cr.at[i, d, l])
        for e in range(1, nx):
            send_x[e - 1, d, l] = pair(d, l, turn(x, e, nx)).astype(bf16)
            send(send_x.at[e - 1, d, l], buf_x.at[e - 1, d, l],
                 xs.at[e - 1, d, l], xr.at[e - 1, d, l], x_peers[e - 1])
        if k == 0:
            peak.relay()
    for k, (d, l) in enumerate(order):
        for e in range(1, nx):
            arrived(buf_x.at[e - 1, d, l], xr.at[e - 1, d, l])
        total = pair(d, l, x)
        for e in range(1, nx):
            total = total + buf_x[e - 1, d, l].astype(f32)
        if d:
            send_z[d - 1, l] = total.astype(bf16)
            send(send_z.at[d - 1, l], buf_z.at[d - 1, l], zs.at[d - 1, l], zr.at[d - 1, l], z_peers[d - 1])
        else:
            own[l] = total
    peaks = peak.finish()

    for l in range(nl):
        total = own[l]
        for d in range(1, nz):
            arrived(buf_z.at[d - 1, l], zr.at[d - 1, l])
            total = total + buf_z[d - 1, l].astype(f32)
        gsum = total / peaks[l]
        first = (decay_first * m1_wide[:, l, :] + (1.0 - decay_first) * gsum).astype(bf16)
        second = decay_second * m2_ref[l] + (1.0 - decay_second) * gsum * gsum
        o1_wide[:, l, :] = first.astype(f32)
        o2_ref[l] = second
        step_dir = first.astype(f32) / bias_first / (jnp.sqrt(second / bias_second) + adam_epsilon)
        master = ms_ref[l]
        fresh = master - learn_rate * (step_dir + weight_decay * master)
        om_ref[l] = fresh
        wg[l, z, x, c] = fresh.astype(bf16)
        wk[0, l] = fold(fresh)
        mine = wg.at[l, z, x, c]
        for d in range(1, nz):
            send(mine, mine, gzs.at[d - 1, l], gzr.at[d - 1, l], z_peers[d - 1])
        for e in range(1, nx):
            send(mine, mine, gxs.at[e - 1, 0, l], gxr.at[e - 1, 0, l], x_peers[e - 1])
        for i in range(1, nc):
            send(mine, mine, gcs.at[i - 1, 0, 0, l], gcr.at[i - 1, 0, 0, l], core_peers[i - 1])
    wpeak = Peak(wk, wk_in, ws, wr)
    wpeak.push(0)
    o1_ref[...] = o1_wide[...].astype(bf16)

    def back(v, d, n):
        return lax.rem(v + n - d, n)

    def from_z(d, l):
        block = wg.at[l, back(z, d, nz), x, c]
        arrived(block, gzr.at[d - 1, l])
        for e in range(1, nx):
            send(block, block, gxs.at[e - 1, d, l], gxr.at[e - 1, d, l], x_peers[e - 1])
        for i in range(1, nc):
            send(block, block, gcs.at[i - 1, 0, d, l], gcr.at[i - 1, 0, d, l], core_peers[i - 1])

    def from_x(d, l):
        for e in range(1, nx):
            block = wg.at[l, back(z, d, nz), back(x, e, nx), c]
            arrived(block, gxr.at[e - 1, d, l])
            for i in range(1, nc):
                send(block, block, gcs.at[i - 1, e, d, l], gcr.at[i - 1, e, d, l], core_peers[i - 1])

    wpeak.relay()
    for d in range(1, nz):
        for l in range(nl):
            from_z(d, l)
        for l in range(nl):
            from_x(d - 1, l)
    for l in range(nl):
        from_x(nz - 1, l)
    peaks = wpeak.finish()
    scales = [1.0 / jnp.full((8, LANES), peaks[l], f32)[:1] for l in range(nl)]

    def norm(zz, xx, cc, l):
        ow_ref[l, zz, xx, cc] = (wg[l, zz, xx, cc].astype(f32) * scales[l]).astype(bf16)

    for l in range(nl):
        for i in range(nz * nx):
            norm(i // nx, i % nx, c, l)
    for d in range(nz):
        for e in range(nx):
            for l in range(nl):
                for i in range(1, nc):
                    block = wg.at[l, back(z, d, nz), back(x, e, nx), back(c, i, nc)]
                    arrived(block, gcr.at[i - 1, e, d, l])
                    norm(back(z, d, nz), back(x, e, nx), back(c, i, nc), l)
    for copy in pending:
        copy.wait_send()


def local(n, nt, grads, moment1, moment2, master):
    nz, nx, nc = split_zero(n)
    nl, rows, width = grads.shape[1:]
    deep = (rows // n) * width // LANES
    dims = (nz, nx, nc, nt, nl)
    g = grads.reshape(nl, n, deep, LANES).reshape(nl, nz, nx, nc, deep, LANES)
    flat = (nl, deep, LANES)
    packed = (deep, nl, LANES)
    peers = nc * nt - 1 + nz * nx - 1
    c1, x1, z1 = max(nc - 1, 1), max(nx - 1, 1), max(nz - 1, 1)
    dma = pltpu.SemaphoreType.DMA
    tile = (nl, 8, LANES)
    vm = pl.BlockSpec(memory_space=pltpu.VMEM)
    sems = [dma((c1, nz, nl))] * 2 + [dma((x1, nz, nl))] * 2 + [dma((z1, nl))] * 2
    sems += [dma((z1, nl))] * 2 + [dma((x1, nz, nl))] * 2 + [dma((c1, nx, nz, nl))] * 2
    sems += [dma((peers,))] * 4
    o1, o2, om, weights = pl.pallas_call(
        functools.partial(kernel, dims),
        out_shape=(
            jax.ShapeDtypeStruct(packed, bf16),
            jax.ShapeDtypeStruct(flat, f32),
            jax.ShapeDtypeStruct(flat, f32),
            jax.ShapeDtypeStruct((nl, nz, nx, nc, deep, LANES), bf16),
        ),
        in_specs=[vm] * 4,
        out_specs=(vm,) * 4,
        scratch_shapes=[
            pltpu.VMEM((nl, nz, nx, nc, deep, LANES), bf16),
            pltpu.VMEM(packed, f32),
            pltpu.VMEM(packed, f32),
            pltpu.VMEM((c1, nz, nl, nx, deep, LANES), bf16),
            pltpu.VMEM((x1, nz) + flat, bf16),
            pltpu.VMEM((x1, nz) + flat, bf16),
            pltpu.VMEM((z1,) + flat, bf16),
            pltpu.VMEM((z1,) + flat, bf16),
            pltpu.VMEM(flat, f32),
            pltpu.VMEM((2,) + tile, f32),
            pltpu.VMEM((peers,) + tile, f32),
            pltpu.VMEM((2,) + tile, f32),
            pltpu.VMEM((peers,) + tile, f32),
        ] + sems,
        compiler_params=pltpu.CompilerParams(collective_id=0, has_side_effects=True, vmem_limit_bytes=16 << 20),
    )(g, moment1.reshape(flat).transpose(1, 0, 2), moment2.reshape(flat), master.reshape(flat))
    shape = moment1.shape
    return (o1.transpose(1, 0, 2).reshape(shape), o2.reshape(shape), om.reshape(shape),
            weights.reshape(nl, rows, width))


def solution(mesh):
    n, nt = mesh.shape["zero"], mesh.shape["tensor"]
    placed = (
        P("zero", None, None, "tensor"),
        P(None, "zero", "tensor"),
        P(None, "zero", "tensor"),
        P(None, "zero", "tensor"),
    )
    return jax.shard_map(
        functools.partial(local, n, nt),
        mesh=mesh,
        in_specs=placed,
        out_specs=(
            P(None, "zero", "tensor"),
            P(None, "zero", "tensor"),
            P(None, "zero", "tensor"),
            P(None, None, "tensor"),
        ),
        check_vma=False,
    )
```

time: 58.3 us -> 43.9 us (0.75)
  Pallas kernels: 44.7 us -> 37.7 us
  local copies, waits for them, and re-layouts: 10.7 us -> 5.4 us
  other arithmetic: 1.91 us -> 0 us
    pallas_call x1, Pallas kernels: 44.7 us -> 37.7 us  [local(): pl.pallas_call(functools.partial(kernel, dims), out_shape=(jax.ShapeDtype...]
    reshape x4 -> x1, local copies, waits for them, and re-layouts: 5.24 us -> 1.58 us  [local(): weights.reshape(nl, rows, width)]
    transpose x1 -> x0, other arithmetic: 1.91 us -> none  [local(): weights = wg.astype(bf16).transpose(1, 0, 2, 3).reshape(nl, rows, width)]
    unnamed x8 -> x10, local copies, waits for them, and re-layouts: 4.67 us -> 3.82 us
    slice x1 -> x0, local copies, waits for them, and re-layouts: 0.8 us -> none  [local(): wg = wg.reshape((n,) + flat).astype(f32) / wp[:, :1, :1][None]]
where the time goes in v2:
time: 43.9 us; the launch traced here: 43.8 us
  Pallas kernels  37.7 us (86%)
  local copies, waits for them, and re-layouts  5.4 us (12%)
  between operations  0.7 us (2%)
    pallas_call x1, Pallas kernels, local(): pl.pallas_call(functools.partial(kernel, dims), out_shape=(jax.ShapeDtype...  37.7 us
    unnamed x10, local copies, waits for them, and re-layouts  3.82 us
    reshape x1, local copies, waits for them, and re-layouts, local(): weights.reshape(nl, rows, width)  1.58 us

profile of v2, /device:TPU:0, one launch (start us, length us, event | category | flops | bytes accessed | tf_op | source)
XLA Modules:
  0.0 43.8 jit_solution(1250713477366930641)
XLA Ops:
  0.6 0.0 copy-start
  0.6 0.0 copy-start.1
  0.7 0.0 copy-start.2
  0.7 1.8 %copy.10 = bf16[4,8,192,128]{3,2,1,0:T(8,128)(2,1)S(1)} copy(bf16[4,8,192,128]{3,1,2,0:T(8,128)(2,1)} %bitcast.24) | data formatting | bytes 3145728
  2.5 0.0 copy-done
  2.5 0.0 copy-done.1
  2.5 0.0 copy-done.2
  2.5 37.7 %shard_map.75 = (bf16[192,2,128]{2,1,0:T(2,128)(2,1)S(1)}, f32[2,192,128]{2,1,0:T(8,128)S(1)}, f32[2,192,128]{2,1,0:T(8,128)S(1)}, bf16[2,4,2,2,192,128]{5,4,3,2,1,0:T(8,128)(2,1)S(1)}) custom-call(bf16[2,4,2,2,192,128]{5,4,3,2,1,0:T(8,128)(2,1)S(1)} %bitcast.17, bf16[192,2,128]{2,1,0:T(2,128)(2,1)S(1)} %bitcast.22, f32[2,192,128]{2,1,0:T(8,128)S(1)} %bitcast.20, ...), custom_call_target="tpu_custom_call" | custom-call | tf_op jit(solution)/shard_map/pallas_call | solution.py:241
  40.2 1.6 %reshape.35 = bf16[2,16,24576]{2,1,0:T(8,128)(2,1)} reshape(bf16[2,4,2,2,192,128]{5,4,3,2,1,0:T(8,128)(2,1)S(1)} %get-tuple-element.11) | data formatting | bytes 3145728 | tf_op jit(solution)/shard_map/reshape | solution.py:270
  41.8 0.6 %copy.14 = bf16[2,1,24576]{2,0,1:T(2,128)(2,1)} copy(bf16[2,1,24576]{2,0,1:T(2,128)(2,1)S(1)} %bitcast.23) | data formatting | bytes 196608
  42.4 0.7 %copy.15 = f32[2,1,24576]{2,1,0:T(1,128)} copy(f32[2,1,24576]{2,1,0:T(1,128)S(1)} %bitcast.19) | data formatting | bytes 393216
  43.1 0.7 %copy.16 = f32[2,1,24576]{2,1,0:T(1,128)} copy(f32[2,1,24576]{2,1,0:T(1,128)S(1)} %bitcast.18) | data formatting | bytes 393216
Async XLA Ops:
  0.6 1.9 %copy-start = (f32[2,1,24576]{2,1,0:T(1,128)S(1)}, f32[2,1,24576]{2,1,0:T(1,128)}, u32[]{:S(2)}) copy-start(f32[2,1,24576]{2,1,0:T(1,128)} %param.6) | copy-start | bytes 589828
  0.6 1.9 %copy-start.1 = (f32[2,1,24576]{2,1,0:T(1,128)S(1)}, f32[2,1,24576]{2,1,0:T(1,128)}, u32[]{:S(2)}) copy-start(f32[2,1,24576]{2,1,0:T(1,128)} %param.7) | copy-start | bytes 589828
  0.7 1.9 %copy-start.2 = (bf16[2,1,24576]{2,0,1:T(2,128)(2,1)S(1)}, bf16[2,1,24576]{2,0,1:T(2,128)(2,1)}, u32[]{:S(2)}) copy-start(bf16[2,1,24576]{2,0,1:T(2,128)(2,1)} %param.5) | copy-start | bytes 294916

commit v3 on v2

v3 whole, which is shorter than its diff:
```python
import functools

import jax
import jax.numpy as jnp
from jax import lax
from jax.experimental import pallas as pl
from jax.experimental.pallas import tpu as pltpu
from jax.sharding import PartitionSpec as P

decay_first = 0.9
decay_second = 0.95
learn_rate = 0.001
weight_decay = 0.1
adam_epsilon = 1e-08
peak_epsilon = 1e-06
bias_first = 1.0 - 0.9**10
bias_second = 1.0 - 0.95**10

LANES = 128
CUTS = 2
MESH = pl.DeviceIdType.MESH
f32 = jnp.float32
bf16 = jnp.bfloat16


def split_zero(n):
    nc = 2 if n % 2 == 0 else 1
    m = n // nc
    nx = 1
    while (nx * 2) * (nx * 2) <= m and m % (nx * 2) == 0:
        nx *= 2
    return m // nx, nx, nc


def fold(block):
    return jnp.max(jnp.abs(block.astype(f32)).reshape(-1, 8, LANES), axis=0)


def kernel(dims, g_ref, m1_ref, m2_ref, ms_ref,
           o1_ref, o2_ref, om_ref, ow_ref,
           wg, m1_wide, o1_wide, buf_c, send_x, buf_x, send_z, buf_z, own,
           pk, pk_in, wk, wk_in,
           cs, cr, xs, xr, zs, zr, gzs, gzr, gxs, gxr, gcs, gcr, ps, pr, ws, wr):
    nz, nx, nc, nt, nl, nh = dims
    nk = nl * nh
    me = lax.axis_index("zero")
    te = lax.axis_index("tensor")
    c = lax.rem(me, nc)
    x = lax.rem(lax.div(me, nc), nx)
    z = lax.div(me, nc * nx)

    def at(zz, xx, cc):
        return {"zero": (zz * nx + xx) * nc + cc}

    def turn(v, d, n):
        return lax.rem(v + d, n)

    core_peers = [at(z, x, turn(c, d, nc)) for d in range(1, nc)]
    x_peers = [at(z, turn(x, d, nx), c) for d in range(1, nx)]
    z_peers = [at(turn(z, d, nz), x, c) for d in range(1, nz)]
    t_peers = [{"tensor": turn(te, d, nt)} for d in range(1, nt)]
    near = core_peers + t_peers + [
        {**at(z, x, turn(c, i, nc)), "tensor": turn(te, d, nt)} for i in range(1, nc) for d in range(1, nt)]
    far = [at(turn(z, d, nz), turn(x, e, nx), c) for d in range(nz) for e in range(nx) if d or e]
    pending = []

    def send(src, dst, s, r, to):
        copy = pltpu.make_async_remote_copy(
            src_ref=src, dst_ref=dst, send_sem=s, recv_sem=r,
            device_id=to, device_id_type=MESH)
        copy.start()
        pending.append(copy)

    def arrived(dst, r):
        pltpu.make_async_copy(dst, dst, r).wait()

    barrier = pltpu.get_barrier_semaphore()
    everyone = near + far
    for p in everyone:
        pl.semaphore_signal(barrier, inc=1, device_id=p, device_id_type=MESH)

    class Peak:
        def __init__(self, held, inbox, s, r):
            self.held, self.inbox, self.s, self.r = held, inbox, s, r

        def push(self, stage):
            first = 0 if stage == 0 else len(near)
            for i, p in enumerate(near if stage == 0 else far):
                k = first + i
                send(self.held.at[stage], self.inbox.at[k], self.s.at[k], self.r.at[k], p)

        def pull(self, stage):
            first = 0 if stage == 0 else len(near)
            best = self.held[stage]
            for k in range(first, first + len(near if stage == 0 else far)):
                arrived(self.inbox.at[k], self.r.at[k])
                best = jnp.maximum(best, self.inbox[k])
            return best

        def relay(self):
            self.held[1] = self.pull(0)
            self.push(1)

        def finish(self):
            best = self.pull(1)
            return [jnp.max(best[l]) + peak_epsilon for l in range(nl)]

    for l in range(nl):
        def part(i, best, l=l):
            zz, rest = lax.div(i, nx * nc), lax.rem(i, nx * nc)
            for h in range(nh):
                best = jnp.maximum(best, fold(g_ref[l, zz, lax.div(rest, nc), lax.rem(rest, nc), h]))
            return best
        pk[0, l] = lax.fori_loop(0, nz * nx * nc, part, jnp.zeros((8, LANES), f32))

    pl.semaphore_wait(barrier, len(everyone))

    peak = Peak(pk, pk_in, ps, pr)
    peak.push(0)
    def pair(d, k, xx):
        total = g_ref[k // nh, turn(z, d, nz), xx, c, k % nh].astype(f32)
        for i in range(nc - 1):
            total = total + buf_c[i, d, k, xx].astype(f32)
        return total

    order = list(range(1, nz)) + [0]

    def swap_cores(k):
        for d in order:
            for i in range(1, nc):
                send(g_ref.at[k // nh, turn(z, d, nz), :, turn(c, i, nc), k % nh], buf_c.at[i - 1, d, k],
                     cs.at[i - 1, d, k], cr.at[i - 1, d, k], core_peers[i - 1])

    def reduce_core(k):
        for d in order:
            for i in range(nc - 1):
                arrived(buf_c.at[i, d, k], cr.at[i, d, k])
            for e in range(1, nx):
                send_x[e - 1, d, k] = pair(d, k, turn(x, e, nx)).astype(bf16)
                send(send_x.at[e - 1, d, k], buf_x.at[e - 1, d, k],
                     xs.at[e - 1, d, k], xr.at[e - 1, d, k], x_peers[e - 1])

    def reduce_x(k):
        for d in order:
            for e in range(1, nx):
                arrived(buf_x.at[e - 1, d, k], xr.at[e - 1, d, k])
            total = pair(d, k, x)
            for e in range(1, nx):
                total = total + buf_x[e - 1, d, k].astype(f32)
            if d:
                send_z[d - 1, k] = total.astype(bf16)
                send(send_z.at[d - 1, k], buf_z.at[d - 1, k], zs.at[d - 1, k], zr.at[d - 1, k], z_peers[d - 1])
            else:
                own[k] = total

    up, down = z < nz - 1, z > 0
    ways = [(up, 1), (down, -1)]

    def came(s, way):
        return z >= s if way == 0 else z + s < nz

    def onward(block, s, way, k):
        go, sign = ways[way]

        @pl.when(go)
        def _():
            hop = pltpu.make_async_remote_copy(
                src_ref=block, dst_ref=block, send_sem=gzs.at[way, s, k], recv_sem=gzr.at[way, s, k],
                device_id=at(z + sign, x, c), device_id_type=MESH)
            hop.start()

    def spread(block, slot, k):
        for e in range(1, nx):
            pltpu.make_async_remote_copy(
                src_ref=block, dst_ref=block, send_sem=gxs.at[e - 1, slot, k], recv_sem=gxr.at[e - 1, slot, k],
                device_id=x_peers[e - 1], device_id_type=MESH).start()
        for i in range(1, nc):
            pltpu.make_async_remote_copy(
                src_ref=block, dst_ref=block, send_sem=gcs.at[i - 1, 0, slot, k],
                recv_sem=gcr.at[i - 1, 0, slot, k],
                device_id=core_peers[i - 1], device_id_type=MESH).start()

    def view(k, zz, xx, cc):
        return wg.at[k // nh, zz, xx, cc, k % nh]

    def source(slot):
        if slot == 0:
            return z
        s, way = (slot + 1) // 2, (slot - 1) % 2
        return z - s if way == 0 else z + s

    def update(k):
        l, h = k // nh, k % nh
        total = own[k]
        for d in range(1, nz):
            arrived(buf_z.at[d - 1, k], zr.at[d - 1, k])
            total = total + buf_z[d - 1, k].astype(f32)
        gsum = total / peaks[l]
        first = (decay_first * m1_wide[h, :, l, :] + (1.0 - decay_first) * gsum).astype(bf16)
        second = decay_second * m2_ref[k] + (1.0 - decay_second) * gsum * gsum
        step_dir = first.astype(f32) / bias_first / (jnp.sqrt(second / bias_second) + adam_epsilon)
        master = ms_ref[k]
        fresh = master - learn_rate * (step_dir + weight_decay * master)
        wg[l, z, x, c, h] = fresh.astype(bf16)
        mine = view(k, z, x, c)
        onward(mine, 0, 0, k)
        onward(mine, 0, 1, k)
        spread(mine, 0, k)
        om_ref[k] = fresh
        o2_ref[k] = second
        o1_wide[h, :, l, :] = first.astype(f32)
        best = fold(fresh)
        wk[0, l] = best if h == 0 else jnp.maximum(wk[0, l], best)

    def gather_z(k, s):
        for way in (0, 1):
            @pl.when(came(s, way))
            def _(way=way):
                slot = 2 * s - 1 + way
                block = view(k, source(slot), x, c)
                arrived(block, gzr.at[way, s - 1, k])
                if s < nz - 1:
                    onward(block, s, way, k)
                spread(block, slot, k)

    def each_slot(s, act):
        if s == 0:
            act(0)
            return
        for way in (0, 1):
            @pl.when(came(s, way))
            def _(way=way):
                act(2 * s - 1 + way)

    def gather_x(k, s):
        def act(slot):
            for e in range(1, nx):
                block = view(k, source(slot), lax.rem(x + nx - e, nx), c)
                arrived(block, gxr.at[e - 1, slot, k])
                for i in range(1, nc):
                    pltpu.make_async_remote_copy(
                        src_ref=block, dst_ref=block, send_sem=gcs.at[i - 1, e, slot, k],
                        recv_sem=gcr.at[i - 1, e, slot, k],
                        device_id=core_peers[i - 1], device_id_type=MESH).start()
        each_slot(s, act)

    for k in range(nk):
        swap_cores(k)
    m1_wide[...] = m1_ref[...].astype(f32)
    reduce_core(0)
    peak.relay()
    for k in range(1, nk):
        reduce_core(k)
    wpeak = Peak(wk, wk_in, ws, wr)
    peaks = []

    def stage(number, k):
        if not 0 <= k < nk:
            return
        if number == 0:
            reduce_x(k)
        elif number == 1:
            if k == 0:
                peaks.extend(peak.finish())
            update(k)
            if k == nk - 1:
                wpeak.push(0)
        elif number == 2:
            gather_z(k, 1)
            gather_x(k, 0)
        else:
            if number == 3 and k == nk - 1:
                wpeak.relay()
            s = number - 1
            if s < nz:
                gather_z(k, s)
            gather_x(k, s - 1)

    last = nz + 1
    for t in range(nk + last + 1):
        for number in range(last, -1, -1):
            stage(number, t - number)
    o1_ref[...] = o1_wide[...].astype(bf16)
    top = wpeak.finish()
    scales = [1.0 / jnp.full((8, LANES), top[l], f32)[:1] for l in range(nl)]

    def norm(l, zz, xx, cc, h):
        ow_ref[l, zz, xx, cc, h] = (wg[l, zz, xx, cc, h].astype(f32) * scales[l]).astype(bf16)

    for k in range(nk):
        for i in range(nz * nx):
            norm(k // nh, i // nx, i % nx, c, k % nh)
    for k in range(nk):
        for s in range(nz):
            def act(slot, k=k):
                for e in range(nx):
                    xx = lax.rem(x + nx - e, nx)
                    for i in range(1, nc):
                        cc = lax.rem(c + nc - i, nc)
                        arrived(view(k, source(slot), xx, cc), gcr.at[i - 1, e, slot, k])
                        norm(k // nh, source(slot), xx, cc, k % nh)
            each_slot(s, act)

    one = view(0, z, x, c)

    def left(sem):
        pltpu.make_async_copy(one, one, sem).wait()

    for k in range(nk):
        for way in (0, 1):
            @pl.when(ways[way][0])
            def _(k=k, way=way):
                left(gzs.at[way, 0, k])
                for s in range(1, nz - 1):
                    @pl.when(came(s, way))
                    def _(s=s):
                        left(gzs.at[way, s, k])
        for s in range(nz):
            def gone(slot, k=k):
                for e in range(1, nx):
                    left(gxs.at[e - 1, slot, k])
                for i in range(1, nc):
                    for e in range(nx):
                        left(gcs.at[i - 1, e, slot, k])
            each_slot(s, gone)
    for copy in pending:
        copy.wait_send()


def local(n, nt, grads, moment1, moment2, master):
    nz, nx, nc = split_zero(n)
    nl, rows, width = grads.shape[1:]
    deep = (rows // n) * width // LANES
    nh = next((h for h in (CUTS, 3, 2) if deep % (16 * h) == 0), 1)
    nk, dh = nl * nh, deep // nh
    dims = (nz, nx, nc, nt, nl, nh)
    whole = (nl, nz, nx, nc, nh, dh, LANES)
    flat = (nk, dh, LANES)
    packed = (nh, dh, nl, LANES)
    peers = nc * nt - 1 + nz * nx - 1
    c1, x1, z1 = max(nc - 1, 1), max(nx - 1, 1), max(nz - 1, 1)
    slots = 2 * nz - 1
    dma = pltpu.SemaphoreType.DMA
    tile = (nl, 8, LANES)
    vm = pl.BlockSpec(memory_space=pltpu.VMEM)
    sems = [dma((c1, nz, nk))] * 2 + [dma((x1, nz, nk))] * 2 + [dma((z1, nk))] * 2
    sems += [dma((2, z1, nk))] * 2 + [dma((x1, slots, nk))] * 2 + [dma((c1, nx, slots, nk))] * 2
    sems += [dma((peers,))] * 4
    o1, o2, om, weights = pl.pallas_call(
        functools.partial(kernel, dims),
        out_shape=(
            jax.ShapeDtypeStruct(packed, bf16),
            jax.ShapeDtypeStruct(flat, f32),
            jax.ShapeDtypeStruct(flat, f32),
            jax.ShapeDtypeStruct(whole, bf16),
        ),
        in_specs=[vm] * 4,
        out_specs=(vm,) * 4,
        scratch_shapes=[
            pltpu.VMEM(whole, bf16),
            pltpu.VMEM(packed, f32),
            pltpu.VMEM(packed, f32),
            pltpu.VMEM((c1, nz, nk, nx, dh, LANES), bf16),
            pltpu.VMEM((x1, nz) + flat, bf16),
            pltpu.VMEM((x1, nz) + flat, bf16),
            pltpu.VMEM((z1,) + flat, bf16),
            pltpu.VMEM((z1,) + flat, bf16),
            pltpu.VMEM(flat, f32),
            pltpu.VMEM((2,) + tile, f32),
            pltpu.VMEM((peers,) + tile, f32),
            pltpu.VMEM((2,) + tile, f32),
            pltpu.VMEM((peers,) + tile, f32),
        ] + sems,
        compiler_params=pltpu.CompilerParams(collective_id=0, has_side_effects=True, vmem_limit_bytes=16 << 20),
    )(grads.reshape(whole), moment1.reshape(nl, nh, dh, LANES).transpose(1, 2, 0, 3),
      moment2.reshape(flat), master.reshape(flat))
    shape = moment1.shape
    return (o1.transpose(2, 0, 1, 3).reshape(shape), o2.reshape(shape), om.reshape(shape),
            weights.reshape(nl, rows, width))


def solution(mesh):
    n, nt = mesh.shape["zero"], mesh.shape["tensor"]
    placed = (
        P("zero", None, None, "tensor"),
        P(None, "zero", "tensor"),
        P(None, "zero", "tensor"),
        P(None, "zero", "tensor"),
    )
    return jax.shard_map(
        functools.partial(local, n, nt),
        mesh=mesh,
        in_specs=placed,
        out_specs=(
            P(None, "zero", "tensor"),
            P(None, "zero", "tensor"),
            P(None, "zero", "tensor"),
            P(None, None, "tensor"),
        ),
        check_vma=False,
    )
```

time: 43.9 us -> 49.8 us (1.13)
  Pallas kernels: 37.7 us -> 43.6 us
    pallas_call x1, Pallas kernels: 37.7 us -> 43.6 us  [local(): pl.pallas_call(functools.partial(kernel, dims), out_shape=(jax.ShapeDtype...]
where the time goes in v3:
time: 49.8 us; the launch traced here: 49.7 us
  Pallas kernels  43.6 us (88%)
  local copies, waits for them, and re-layouts  5.4 us (11%)
  between operations  0.7 us (1%)
    pallas_call x1, Pallas kernels, local(): pl.pallas_call(functools.partial(kernel, dims), out_shape=(jax.ShapeDtype...  43.6 us
    unnamed x10, local copies, waits for them, and re-layouts  3.82 us
    reshape x1, local copies, waits for them, and re-layouts, local(): weights.reshape(nl, rows, width)  1.58 us

profile of v3, /device:TPU:0, one launch (start us, length us, event | category | flops | bytes accessed | tf_op | source)
XLA Modules:
  0.0 49.7 jit_solution(3266660293570968451)
XLA Ops:
  0.6 0.0 copy-start
  0.6 0.0 copy-start.1
  0.7 0.0 copy-start.2
  0.7 1.8 %copy.10 = bf16[4,8,192,128]{3,2,1,0:T(8,128)(2,1)S(1)} copy(bf16[4,8,192,128]{3,1,2,0:T(8,128)(2,1)} %bitcast.24) | data formatting | bytes 3145728
  2.5 0.0 copy-done
  2.5 0.0 copy-done.1
  2.5 0.0 copy-done.2
  2.5 43.6 %shard_map.75 = (bf16[2,96,2,128]{3,2,1,0:T(2,128)(2,1)S(1)}, f32[4,96,128]{2,1,0:T(8,128)S(1)}, f32[4,96,128]{2,1,0:T(8,128)S(1)}, bf16[2,4,2,2,2,96,128]{6,5,4,3,2,1,0:T(8,128)(2,1)S(1)}) custom-call(bf16[2,4,2,2,2,96,128]{6,5,4,3,2,1,0:T(8,128)(2,1)S(1)} %bitcast.17, bf16[2,96,2,128]{3,2,1,0:T(2,128)(2,1)S(1)} %bitcast.22, f32[4,96,128]{2,1,0:T(8,128)S(1)} %bitcast.20, ...), custom_call_target="tpu_custom_call" | custom-call | tf_op jit(solution)/shard_map/pallas_call | solution.py:349
  46.1 1.6 %reshape.39 = bf16[2,16,24576]{2,1,0:T(8,128)(2,1)} reshape(bf16[2,4,2,2,2,96,128]{6,5,4,3,2,1,0:T(8,128)(2,1)S(1)} %get-tuple-element.11) | data formatting | bytes 3145728 | tf_op jit(solution)/shard_map/reshape | solution.py:379
  47.7 0.6 %copy.14 = bf16[2,1,24576]{2,0,1:T(2,128)(2,1)} copy(bf16[2,1,24576]{2,0,1:T(2,128)(2,1)S(1)} %bitcast.23) | data formatting | bytes 196608
  48.3 0.7 %copy.15 = f32[2,1,24576]{2,1,0:T(1,128)} copy(f32[2,1,24576]{2,1,0:T(1,128)S(1)} %bitcast.19) | data formatting | bytes 393216
  49.0 0.7 %copy.16 = f32[2,1,24576]{2,1,0:T(1,128)} copy(f32[2,1,24576]{2,1,0:T(1,128)S(1)} %bitcast.18) | data formatting | bytes 393216
Async XLA Ops:
  0.6 1.9 %copy-start = (f32[2,1,24576]{2,1,0:T(1,128)S(1)}, f32[2,1,24576]{2,1,0:T(1,128)}, u32[]{:S(2)}) copy-start(f32[2,1,24576]{2,1,0:T(1,128)} %param.6) | copy-start | bytes 589828
  0.6 1.9 %copy-start.1 = (f32[2,1,24576]{2,1,0:T(1,128)S(1)}, f32[2,1,24576]{2,1,0:T(1,128)}, u32[]{:S(2)}) copy-start(f32[2,1,24576]{2,1,0:T(1,128)} %param.7) | copy-start | bytes 589828
  0.7 1.9 %copy-start.2 = (bf16[2,1,24576]{2,0,1:T(2,128)(2,1)S(1)}, bf16[2,1,24576]{2,0,1:T(2,128)(2,1)}, u32[]{:S(2)}) copy-start(bf16[2,1,24576]{2,0,1:T(2,128)(2,1)} %param.5) | copy-start | bytes 294916

commit v4 on v3

--- a/solution.py
+++ b/solution.py
@@ -17,7 +17,8 @@
 bias_second = 1.0 - 0.95**10
 
 LANES = 128
-CUTS = 2
+CUTS = 1
+STEP, LAG, HOP = 8.4, 20, 20
 MESH = pl.DeviceIdType.MESH
 f32 = jnp.float32
 bf16 = jnp.bfloat16
@@ -174,11 +175,9 @@
             pltpu.make_async_remote_copy(
                 src_ref=block, dst_ref=block, send_sem=gxs.at[e - 1, slot, k], recv_sem=gxr.at[e - 1, slot, k],
                 device_id=x_peers[e - 1], device_id_type=MESH).start()
-        for i in range(1, nc):
-            pltpu.make_async_remote_copy(
-                src_ref=block, dst_ref=block, send_sem=gcs.at[i - 1, 0, slot, k],
-                recv_sem=gcr.at[i - 1, 0, slot, k],
-                device_id=core_peers[i - 1], device_id_type=MESH).start()
+
+    def line(k, zz, cc):
+        return wg.at[k // nh, zz, :, cc, k % nh]
 
     def view(k, zz, xx, cc):
         return wg.at[k // nh, zz, xx, cc, k % nh]
@@ -237,11 +236,12 @@
             for e in range(1, nx):
                 block = view(k, source(slot), lax.rem(x + nx - e, nx), c)
                 arrived(block, gxr.at[e - 1, slot, k])
-                for i in range(1, nc):
-                    pltpu.make_async_remote_copy(
-                        src_ref=block, dst_ref=block, send_sem=gcs.at[i - 1, e, slot, k],
-                        recv_sem=gcr.at[i - 1, e, slot, k],
-                        device_id=core_peers[i - 1], device_id_type=MESH).start()
+            blocks = line(k, source(slot), c)
+            for i in range(1, nc):
+                pltpu.make_async_remote_copy(
+                    src_ref=blocks, dst_ref=blocks, send_sem=gcs.at[i - 1, slot, k],
+                    recv_sem=gcr.at[i - 1, slot, k],
+                    device_id=core_peers[i - 1], device_id_type=MESH).start()
         each_slot(s, act)
 
     for k in range(nk):
@@ -276,10 +276,13 @@
                 gather_z(k, s)
             gather_x(k, s - 1)
 
-    last = nz + 1
-    for t in range(nk + last + 1):
-        for number in range(last, -1, -1):
-            stage(number, t - number)
+    due = []
+    for k in range(nk):
+        begun = STEP * k / nk
+        for number in range(nz + 2):
+            due.append((begun + (LAG + HOP * (number - 1) if number else 0), k, number))
+    for _, k, number in sorted(due):
+        stage(number, k)
     o1_ref[...] = o1_wide[...].astype(bf16)
     top = wpeak.finish()
     scales = [1.0 / jnp.full((8, LANES), top[l], f32)[:1] for l in range(nl)]
@@ -293,11 +296,10 @@
     for k in range(nk):
         for s in range(nz):
             def act(slot, k=k):
-                for e in range(nx):
-                    xx = lax.rem(x + nx - e, nx)
-                    for i in range(1, nc):
-                        cc = lax.rem(c + nc - i, nc)
-                        arrived(view(k, source(slot), xx, cc), gcr.at[i - 1, e, slot, k])
+                for i in range(1, nc):
+                    cc = lax.rem(c + nc - i, nc)
+                    arrived(line(k, source(slot), cc), gcr.at[i - 1, slot, k])
+                    for xx in range(nx):
                         norm(k // nh, source(slot), xx, cc, k % nh)
             each_slot(s, act)
 
@@ -320,11 +322,17 @@
                 for e in range(1, nx):
                     left(gxs.at[e - 1, slot, k])
                 for i in range(1, nc):
-                    for e in range(nx):
-                        left(gcs.at[i - 1, e, slot, k])
+                    lot = line(0, z, c)
+                    pltpu.make_async_copy(lot, lot, gcs.at[i - 1, slot, k]).wait()
             each_slot(s, gone)
     for copy in pending:
         copy.wait_send()
+
+
+def hand_on(a_ref, b_ref, c_ref, x_ref, y_ref, z_ref):
+    x_ref[...] = a_ref[...]
+    y_ref[...] = b_ref[...]
+    z_ref[...] = c_ref[...]
 
 
 def local(n, nt, grads, moment1, moment2, master):
@@ -344,7 +352,7 @@
     tile = (nl, 8, LANES)
     vm = pl.BlockSpec(memory_space=pltpu.VMEM)
     sems = [dma((c1, nz, nk))] * 2 + [dma((x1, nz, nk))] * 2 + [dma((z1, nk))] * 2
-    sems += [dma((2, z1, nk))] * 2 + [dma((x1, slots, nk))] * 2 + [dma((c1, nx, slots, nk))] * 2
+    sems += [dma((2, z1, nk))] * 2 + [dma((x1, slots, nk))] * 2 + [dma((c1, slots, nk))] * 2
     sems += [dma((peers,))] * 4
     o1, o2, om, weights = pl.pallas_call(
         functools.partial(kernel, dims),
@@ -374,6 +382,13 @@
         compiler_params=pltpu.CompilerParams(collective_id=0, has_side_effects=True, vmem_limit_bytes=16 << 20),
     )(grads.reshape(whole), moment1.reshape(nl, nh, dh, LANES).transpose(1, 2, 0, 3),
       moment2.reshape(flat), master.reshape(flat))
+    o1, o2, om = pl.pallas_call(
+        hand_on,
+        out_shape=tuple(jax.ShapeDtypeStruct(v.shape, v.dtype) for v in (o1, o2, om)),
+        in_specs=[vm] * 3,
+        out_specs=(vm,) * 3,
+        compiler_params=pltpu.CompilerParams(vmem_limit_bytes=4 << 20),
+    )(o1, o2, om)
     shape = moment1.shape
     return (o1.transpose(2, 0, 1, 3).reshape(shape), o2.reshape(shape), om.reshape(shape),
             weights.reshape(nl, rows, width))

time: 49.8 us -> 42.1 us (0.85)
  Pallas kernels: 43.6 us -> 37.8 us
  local copies, waits for them, and re-layouts: 5.4 us -> 3.39 us
    pallas_call x1, Pallas kernels: 43.6 us -> 37 us  [local(): pl.pallas_call(functools.partial(kernel, dims), out_shape=(jax.ShapeDtype...]
    unnamed x10 -> x7, local copies, waits for them, and re-layouts: 3.82 us -> 1.83 us
    pallas_call x0 -> x1, Pallas kernels: none -> 0.81 us  [local(): pl.pallas_call(hand_on, out_shape=tuple((jax.ShapeDtypeStruct(v.shape, v....]
where the time goes in v4:
time: 42.1 us; the launch traced here: 41.9 us
  Pallas kernels  37.8 us (90%)
  local copies, waits for them, and re-layouts  3.39 us (8%)
  between operations  0.7 us (2%)
    pallas_call x1, Pallas kernels, local(): pl.pallas_call(functools.partial(kernel, dims), out_shape=(jax.ShapeDtype...  37 us
    unnamed x7, local copies, waits for them, and re-layouts  1.83 us
    reshape x1, local copies, waits for them, and re-layouts, local(): weights.reshape(nl, rows, width)  1.56 us

profile of v4, /device:TPU:0, one launch (start us, length us, event | category | flops | bytes accessed | tf_op | source)
XLA Modules:
  0.0 41.9 jit_solution(18342936002454379734)
XLA Ops:
  0.6 0.0 copy-start
  0.6 0.0 copy-start.1
  0.7 0.0 copy-start.2
  0.7 1.8 %copy.10 = bf16[4,8,192,128]{3,2,1,0:T(8,128)(2,1)S(1)} copy(bf16[4,8,192,128]{3,1,2,0:T(8,128)(2,1)} %bitcast.21) | data formatting | bytes 3145728
  2.5 0.0 copy-done
  2.5 0.0 copy-done.1
  2.5 0.0 copy-done.2
  2.5 37.0 %shard_map.75 = (bf16[1,192,2,128]{3,2,1,0:T(2,128)(2,1)S(1)}, f32[2,192,128]{2,1,0:T(8,128)S(1)}, f32[2,192,128]{2,1,0:T(8,128)S(1)}, bf16[2,4,2,2,1,192,128]{6,5,4,3,2,1,0:T(8,128)(2,1)S(1)}) custom-call(bf16[2,4,2,2,1,192,128]{6,5,4,3,2,1,0:T(8,128)(2,1)S(1)} %bitcast.17, bf16[1,192,2,128]{3,2,1,0:T(2,128)(2,1)S(1)} %bitcast.20, ...), custom_call_target="tpu_custom_call" | custom-call | tf_op jit(solution)/shard_map/pallas_call | solution.py:357
  39.5 0.8 %shard_map.76 = (bf16[1,192,2,128]{3,2,1,0:T(2,128)(2,1)}, f32[2,192,128]{2,1,0:T(8,128)}, f32[2,192,128]{2,1,0:T(8,128)}) custom-call(bf16[1,192,2,128]{3,2,1,0:T(2,128)(2,1)S(1)} %get-tuple-element.11.a_ref, f32[2,192,128]{2,1,0:T(8,128)S(1)} %get-tuple-element.12.b_ref, f32[2,192,128]{2,1,0:T(8,128)S(1)} %get-tuple-element.13.c_ref), custom_call_target="tpu_custom_call" | custom-call | tf_op jit(solution)/shard_map/pallas_call | solution.py:385
  40.4 1.6 %reshape.39 = bf16[2,16,24576]{2,1,0:T(8,128)(2,1)} reshape(bf16[2,4,2,2,1,192,128]{6,5,4,3,2,1,0:T(8,128)(2,1)S(1)} %get-tuple-element.17) | data formatting | bytes 3145728 | tf_op jit(solution)/shard_map/reshape | solution.py:394
Async XLA Ops:
  0.6 1.9 %copy-start = (f32[2,1,24576]{2,1,0:T(1,128)S(1)}, f32[2,1,24576]{2,1,0:T(1,128)}, u32[]{:S(2)}) copy-start(f32[2,1,24576]{2,1,0:T(1,128)} %param.6) | copy-start | bytes 589828
  0.6 1.9 %copy-start.1 = (f32[2,1,24576]{2,1,0:T(1,128)S(1)}, f32[2,1,24576]{2,1,0:T(1,128)}, u32[]{:S(2)}) copy-start(f32[2,1,24576]{2,1,0:T(1,128)} %param.7) | copy-start | bytes 589828
  0.7 1.9 %copy-start.2 = (bf16[2,1,24576]{2,0,1:T(2,128)(2,1)S(1)}, bf16[2,1,24576]{2,0,1:T(2,128)(2,1)}, u32[]{:S(2)}) copy-start(bf16[2,1,24576]{2,0,1:T(2,128)(2,1)} %param.5) | copy-start | bytes 294916
